TPU v7x, 512 devices: a whole 4x8x8 slice. The times are simulated.
512 devices in a mesh: dp: 32 (over x, y), tensor: 16 (over z, core).
Axes of the slice: x: 4, y: 8, z: 8, core: 2. Of those that a mesh axis runs over, the one named last changes fastest.
Arguments:
- queries: bfloat16 [4096, 16384], P('dp', 'tensor'), may hold values from -24 to 24
- draft_keys: bfloat16 [4096, 1024], P('dp'), may hold values from -6 to 6
- draft_values: bfloat16 [4096, 1024], P('dp'), may hold values from -6 to 6
- cache_keys: bfloat16 [64, 2048, 1024], P('dp', 'tensor'), may hold values from -24 to 24
- cache_values: bfloat16 [64, 2048, 1024], P('dp', 'tensor'), may hold values from -6 to 6
- out_weight: bfloat16 [16384, 16384], P('tensor', 'dp'), may hold values from -0.25 to 0.25
- cache_lengths: int32 [64], P('dp'), may hold values from 512 to 2048
- draft_lengths: int32 [64], replicated, may hold values from 8 to 64
- dest_group: int32 [64], replicated, may hold values from 0 to 31, as said below
- dest_offset: int32 [64], replicated, may hold values from 0 to 32, as said below
Outputs:
- verified: bfloat16 [3072, 16384], P('tensor', 'dp')
Inputs may be any that keep to these rules, and one draw needn't show every extreme that they name: `dest_group`: at most one request of a group has another group as destination, and each group receives at most one such request. `dest_offset`: blocks with the same destination never intersect and end at packed row 96 or before; a block moved to another group starts right after that group's own rows; in every draw some group's blocks fill all 96 rows.
All inputs are finite; a program needn't handle non-finite values.
Results may differ from a plain program's by a relative error of at most 0.017.
Values may be sent and summed in bfloat16 or wider, within the bound.
No kernel may reach another device: no remote copies, remote signals or barrier semaphores. Data moves between devices by JAX's collectives and lax.ppermute only.
A program may use at most 64 MiB of HBM per device.

v0:
```python
import jax
import jax.numpy as jnp
from jax import lax
from jax.sharding import PartitionSpec as P

HEADS = 128
KV_HEADS = 8
HEAD_DIM = 128
DRAFT = 64
GROUP_REQ = 2
PACK = 96
NEG_FILL = -1e30


def packed_sources(row_ids, draft_lengths, dest_group, dest_offset):
    request_ids = jnp.arange(dest_group.shape[0], dtype=jnp.int32)
    slot_group = row_ids // PACK
    slot_index = row_ids % PACK
    inside = (
        (dest_group[None, :] == slot_group[:, None])
        & (slot_index[:, None] >= dest_offset[None, :])
        & (slot_index[:, None] < (dest_offset + draft_lengths)[None, :])
    )
    request = jnp.sum(jnp.where(inside, request_ids[None, :], 0), axis=1)
    first_slot = jnp.sum(jnp.where(inside, dest_offset[None, :], 0), axis=1)
    return (request, slot_index - first_slot, jnp.any(inside, axis=1))


def attend_one(operands):
    queries_one, cache_k, cache_v, draft_k, draft_v, cache_len, draft_len = operands
    score_scale = HEAD_DIM ** (-0.5)
    cache_scores = (
        jnp.einsum("qkgd,lkd->kgql", queries_one, cache_k, preferred_element_type=jnp.float32)
        * score_scale
    )
    draft_scores = (
        jnp.einsum("qkgd,jkd->kgqj", queries_one, draft_k, preferred_element_type=jnp.float32)
        * score_scale
    )
    cache_pos = jnp.arange(cache_k.shape[0], dtype=jnp.int32)
    draft_pos = jnp.arange(draft_k.shape[0], dtype=jnp.int32)
    keep_cache = cache_pos < cache_len
    keep_draft = (draft_pos[None, :] <= draft_pos[:, None]) & (draft_pos[None, :] < draft_len)
    cache_scores = jnp.where(keep_cache, cache_scores, NEG_FILL)
    draft_scores = jnp.where(keep_draft, draft_scores, NEG_FILL)
    highest = jnp.maximum(
        jnp.max(cache_scores, axis=-1, keepdims=True), jnp.max(draft_scores, axis=-1, keepdims=True)
    )
    cache_exp = jnp.exp(cache_scores - highest)
    draft_exp = jnp.exp(draft_scores - highest)
    denominator = jnp.sum(cache_exp, axis=-1, keepdims=True) + jnp.sum(
        draft_exp, axis=-1, keepdims=True
    )
    cache_weights = (cache_exp / denominator).astype(jnp.bfloat16)
    draft_weights = (draft_exp / denominator).astype(jnp.bfloat16)
    mixed = jnp.einsum("kgql,lkd->qkgd", cache_weights, cache_v, preferred_element_type=jnp.float32)
    mixed = mixed + jnp.einsum(
        "kgqj,jkd->qkgd", draft_weights, draft_v, preferred_element_type=jnp.float32
    )
    is_live = draft_pos < draft_len
    return jnp.where(is_live[:, None, None, None], mixed, 0.0).astype(jnp.bfloat16)


def body(
    queries,
    draft_keys,
    draft_values,
    cache_keys,
    cache_values,
    out_weight,
    cache_lengths,
    draft_lengths,
    dest_group,
    dest_offset,
):
    tensor_count = lax.axis_size("tensor")
    data_count = lax.axis_size("dp")
    my_rank = lax.axis_index("tensor")
    my_group = lax.axis_index("dp")
    local_heads = HEADS // tensor_count
    group_heads = HEADS // KV_HEADS
    kv_local = max(1, local_heads // group_heads)
    per_kv = local_heads // kv_local
    kv_width = kv_local * HEAD_DIM
    span_rows = cache_keys.shape[1]
    copies = tensor_count // KV_HEADS

    def spread(cache_block):
        return jnp.repeat(
            cache_block.reshape(GROUP_REQ, span_rows, KV_HEADS, HEAD_DIM), copies, axis=2
        )

    full_keys, full_values = (
        lax.all_to_all(spread(cache_keys), "tensor", split_axis=2, concat_axis=1, tiled=True),
        lax.all_to_all(spread(cache_values), "tensor", split_axis=2, concat_axis=1, tiled=True),
    )
    kv_first = my_rank * local_heads // group_heads
    draft_k = lax.dynamic_slice_in_dim(draft_keys, kv_first * HEAD_DIM, kv_width, 1).reshape(
        GROUP_REQ, DRAFT, kv_local, HEAD_DIM
    )
    draft_v = lax.dynamic_slice_in_dim(draft_values, kv_first * HEAD_DIM, kv_width, 1).reshape(
        GROUP_REQ, DRAFT, kv_local, HEAD_DIM
    )
    local_queries = queries.reshape(GROUP_REQ, DRAFT, kv_local, per_kv, HEAD_DIM)
    my_lengths = lax.dynamic_slice_in_dim(draft_lengths, my_group * GROUP_REQ, GROUP_REQ)
    attended = lax.map(
        attend_one,
        (local_queries, full_keys, full_values, draft_k, draft_v, cache_lengths, my_lengths),
    )
    width_local = local_heads * HEAD_DIM
    attended_rows = attended.reshape(GROUP_REQ * DRAFT, width_local)
    target_rows = PACK * data_count // tensor_count
    home_all = lax.all_gather(attended_rows, "dp", axis=0, tiled=True)
    row_ids = jnp.arange(lax.axis_size("tensor") * target_rows, dtype=jnp.int32)
    request, within, is_live = packed_sources(row_ids, draft_lengths, dest_group, dest_offset)
    picked = jnp.take(home_all, request * DRAFT + within, axis=0)
    picked = jnp.where(is_live[:, None], picked, jnp.zeros((), jnp.bfloat16))
    return lax.psum_scatter(
        jnp.dot(picked, out_weight, preferred_element_type=jnp.float32).astype(jnp.bfloat16),
        "tensor",
        scatter_dimension=0,
        tiled=True,
    )


def solution(mesh):
    in_specs = (
        P("dp", "tensor"),
        P("dp", None),
        P("dp", None),
        P("dp", "tensor", None),
        P("dp", "tensor", None),
        P("tensor", "dp"),
        P("dp"),
        P(),
        P(),
        P(),
    )
    out_specs = P("tensor", "dp")
    return jax.shard_map(body, mesh=mesh, in_specs=in_specs, out_specs=out_specs, check_vma=False)
```

profile of v0, /device:TPU:8, one launch (start us, length us, event | category | flops | bytes accessed | tf_op | source)
XLA Modules:
  0.0 296.0 jit_solution(7023909836648568548)
XLA Ops:
  6.5 1.3 copy_bitcast_fusion.3
  7.9 1.2 broadcast_in_dim.102
  9.1 10.4 %all-to-all-start.1 = ((bf16[2,128,16,128]{3,1,0,2:T(8,128)(2,1)}), bf16[2,128,16,128]{3,1,0,2:T(8,128)(2,1)S(1)}, u32[]{:S(2)}, u32[]{:S(2)}) async-start(bf16[2,128,16,128]{3,1,0,2:T(8,128)(2,1)} %bitcast.25), calls=%async_computation.1 | async-start | bytes 2097152 | tf_op jit(solution)/shard_map/all_to_all | solution.py:94
  19.5 0.1 copy_bitcast_fusion.4
  19.7 26.3 %all-to-all-done.1 = bf16[2,128,16,128]{3,1,0,2:T(8,128)(2,1)S(1)} async-done(((bf16[2,128,16,128]{3,1,0,2:T(8,128)(2,1)}), bf16[2,128,16,128]{3,1,0,2:T(8,128)(2,1)S(1)}, u32[]{:S(2)}, u32[]{:S(2)}) %all-to-all-start.1) | async-done | bytes 1048608 | tf_op jit(solution)/shard_map/all_to_all | solution.py:94
  46.0 1.3 broadcast_in_dim.101
  47.3 5.0 %all-to-all-start = ((bf16[2,128,16,128]{3,1,0,2:T(8,128)(2,1)}), bf16[2,128,16,128]{3,1,0,2:T(8,128)(2,1)}, u32[]{:S(2)}, u32[]{:S(2)}) async-start(bf16[2,128,16,128]{3,1,0,2:T(8,128)(2,1)} %bitcast.20), calls=%async_computation | async-start | bytes 2097152 | tf_op jit(solution)/shard_map/all_to_all | solution.py:95
  52.3 0.0 all-gather.2.cloned.1.call-start
  52.4 0.1 dynamic_slice.34
  52.5 0.8 constant_dynamic-slice_fusion.1
  53.3 0.1 copy.38
  53.4 25.4 %all-to-all-done = bf16[2,128,16,128]{3,1,0,2:T(8,128)(2,1)} async-done(((bf16[2,128,16,128]{3,1,0,2:T(8,128)(2,1)}), bf16[2,128,16,128]{3,1,0,2:T(8,128)(2,1)}, u32[]{:S(2)}, u32[]{:S(2)}) %all-to-all-start) | async-done | bytes 1048608 | tf_op jit(solution)/shard_map/all_to_all | solution.py:95
  78.8 1.3 copy.36
  80.1 14.2 %while.10 = (s32[]{:T(128)}, bf16[2,64,1,8,128]{4,3,1,0,2:T(8,128)(2,1)}, s32[2]{0:T(128)S(1)}, bf16[2,2048,1,128]{3,1,2,0:T(8,128)(2,1)S(1)}, s32[2]{0:T(128)S(...) while((s32[]{:T(128)}, ...), condition=%wide.region_8.9_spmd, body=%wide.region_3.8_spmd.sunk | while | flops 566699072 | bytes 15692581 | solution.py:106
  80.1 0.7 dynamic_slice.73
  80.8 0.7 iota_compare_fusion.6
  81.5 0.7 dynamic_slice.72
  82.2 0.7 iota_compare_fusion.5
  82.9 0.1 fusion.69
  83.0 0.3 fusion.70
  83.2 0.9 bitcast_reduce_fusion.2
  84.1 0.1 fusion.72
  84.2 0.9 fusion.71
  85.1 1.1 fusion.73
  86.2 0.2 fusion.74
  86.5 0.7 copy_dynamic-update-slice_fusion.2
  87.2 0.7 dynamic_slice.73
  87.9 0.7 iota_compare_fusion.6
  88.6 0.7 dynamic_slice.72
  89.3 0.7 iota_compare_fusion.5
  90.0 0.1 fusion.69
  90.0 0.3 fusion.70
  90.3 0.9 bitcast_reduce_fusion.2
  91.2 0.1 fusion.72
  91.3 0.9 fusion.71
  92.2 1.1 fusion.73
  93.3 0.2 fusion.74
  93.6 0.7 copy_dynamic-update-slice_fusion.2
  94.3 1.7 copy.62
  96.0 0.0 all-gather.2.cloned.1.call-update
  96.0 0.0 reduce-scatter.2.cloned.1.call-start
  96.1 0.4 fusion.50
  96.5 0.4 select_reduce_fusion
  96.9 0.1 compare_select_fusion
  97.0 99.9 %all-gather.2.cloned.1.call-done = bf16[4096,1024]{1,0:T(8,128)(2,1)} async-done(((bf16[128,1024]{1,0:T(8,128)(2,1)}), bf16[4096,1024]{1,0:T(8,128)(2,1)}) %all-gather.2.cloned.1.call-update) | async-done | bytes 8388624 | tf_op jit(solution)/shard_map/all_gather | solution.py:113
  196.9 20.4 %gather_fusion = bf16[3072,1024]{1,0:T(8,128)(2,1)} fusion(bf16[4096,1024]{1,0:T(8,128)(2,1)} %all-gather.2.cloned.1.call-done, s32[3072]{0:T(1024)S(1)} %broadcast_clamp_fusion), kind=kCustom, calls=%fused_computation | custom fusion | bytes 12595200 | tf_op jit(solution)/shard_map/jit(_take)/gather | solution.py:116
  217.3 7.6 %fusion.34 = bf16[3072,512]{1,0:T(8,128)(2,1)} fusion(bf16[1024,512]{1,0:T(8,128)(2,1)S(1)} %copy-done, bf16[3072,1024]{1,0:T(8,128)(2,1)} %gather_fusion, pred[3072]{0:T(1024)(128)(4,1)S(1)} %compare_and_fusion.1, pred[3072]{0:T(1024)(128)(4,1)S(1)} %fusion.50), kind=kOutput, calls=%fused_computation.49 | convolution fusion | flops 3229089792 | bytes 10491904 | tf_op jit(solution)/shard_map/dot_general | solution.py:119
  224.9 64.2 %reduce-scatter.2.cloned.1.call-done = bf16[192,512]{1,0:T(8,128)(2,1)} async-done(((bf16[3072,512]{1,0:T(8,128)(2,1)}), bf16[192,512]{1,0:T(8,128)(2,1)}) %reduce-scatter.2.cloned.1.call-update) | async-done | bytes 196624 | tf_op jit(solution)/shard_map/reduce_scatter | solution.py:118
  (28 shorter events, 0.2 us)
Async XLA Ops:
  6.5 210.7 %copy-start = (bf16[1024,512]{1,0:T(8,128)(2,1)S(1)}, bf16[1024,512]{1,0:T(8,128)(2,1)}, u32[]{:S(2)}) copy-start(bf16[1024,512]{1,0:T(8,128)(2,1)} %param.17) | copy-start | bytes 3145732
  6.5 13.0 %copy-start.1 = (bf16[2,128,1024]{2,1,0:T(8,128)(2,1)S(1)}, bf16[2,128,1024]{2,1,0:T(8,128)(2,1)}, u32[]{:S(2)}) copy-start(bf16[2,128,1024]{2,1,0:T(8,128)(2,1)} %param.16) | copy-start | bytes 1572868
  7.8 44.5 %copy-start.2 = (bf16[128,1024]{1,0:T(8,128)(2,1)S(1)}, bf16[128,1024]{1,0:T(8,128)(2,1)}, u32[]{:S(2)}) copy-start(bf16[128,1024]{1,0:T(8,128)(2,1)} %param.12) | copy-start | bytes 786436
  7.8 44.6 %copy-start.6 = (s32[64]{0:T(128)S(1)}, s32[64]{0:T(128)}, u32[]{:S(2)}) copy-start(s32[64]{0:T(128)} %param.19) | copy-start | bytes 772
  9.1 36.9 %all-to-all-start.1 = ((bf16[2,128,16,128]{3,1,0,2:T(8,128)(2,1)}), bf16[2,128,16,128]{3,1,0,2:T(8,128)(2,1)S(1)}, u32[]{:S(2)}, u32[]{:S(2)}) async-start(bf16[2,128,16,128]{3,1,0,2:T(8,128)(2,1)} %bitcast.25), calls=%async_computation.1 | async-start | bytes 2097152 | tf_op jit(solution)/shard_map/all_to_all | solution.py:94
  19.7 60.4 %copy-start.5 = (s32[2]{0:T(128)S(1)}, s32[2]{0:T(128)}, u32[]{:S(2)}) copy-start(s32[2]{0:T(128)} %param.18) | copy-start | bytes 28
  47.3 31.5 %all-to-all-start = ((bf16[2,128,16,128]{3,1,0,2:T(8,128)(2,1)}), bf16[2,128,16,128]{3,1,0,2:T(8,128)(2,1)}, u32[]{:S(2)}, u32[]{:S(2)}) async-start(bf16[2,128,16,128]{3,1,0,2:T(8,128)(2,1)} %bitcast.20), calls=%async_computation | async-start | bytes 2097152 | tf_op jit(solution)/shard_map/all_to_all | solution.py:95
  52.3 144.6 %all-gather.2.cloned.1.call-start = ((), (), s32[]{:S(2)}) async-start(), calls=%async_computation.3 | async-start | bytes 8650752 | tf_op jit(solution)/shard_map/all_gather | solution.py:113
  80.1 16.0 %copy-start.3 = (s32[64]{0:T(128)S(1)}, s32[64]{0:T(128)}, u32[]{:S(2)}) copy-start(s32[64]{0:T(128)} %param.21) | copy-start | bytes 772
  80.1 16.0 %copy-start.4 = (s32[64]{0:T(128)S(1)}, s32[64]{0:T(128)}, u32[]{:S(2)}) copy-start(s32[64]{0:T(128)} %param.20) | copy-start | bytes 772
  96.0 193.2 %reduce-scatter.2.cloned.1.call-start = ((), (), s32[]{:S(2)}) async-start(), calls=%async_computation.4 | async-start | bytes 3342336 | tf_op jit(solution)/shard_map/reduce_scatter | solution.py:118
Sparse Core Ops, SparseCore 0:
  96.1 100.6 all-gather.1
  225.1 64.0 reduce-scatter.1
where the time goes:
time: 297 us; the launch traced here: 296 us
  waiting for transfers between devices  216 us (73%)
  local copies, waits for them, and re-layouts  32.5 us (11%)
  starting transfers between devices  15.5 us (5%)
  between operations  13.6 us (5%)
  matrix products  12.5 us (4%)
  other arithmetic  5.82 us (2%)
    all_gather x1, waiting for transfers between devices, body(): home_all = lax.all_gather(attended_rows, 'dp', axis=0, tiled=True)  99.9 us
    reduce_scatter x1, waiting for transfers between devices, body(): lax.psum_scatter(jnp.dot(picked, out_weight, preferred_element_type=jnp.f...  64.2 us
    all_to_all x1, waiting for transfers between devices, body(): lax.all_to_all(spread(cache_keys), 'tensor', split_axis=2, concat_axis=1,...  26.3 us
    all_to_all x1, waiting for transfers between devices, body(): lax.all_to_all(spread(cache_values), 'tensor', split_axis=2, concat_axis=...  25.4 us
    gather x1, local copies, waits for them, and re-layouts, body(): picked = jnp.take(home_all, request * DRAFT + within, axis=0)  20.4 us
    all_to_all x1, starting transfers between devices, body(): lax.all_to_all(spread(cache_keys), 'tensor', split_axis=2, concat_axis=1,...  10.4 us
    dot_general x1, matrix products, body(): jnp.dot(picked, out_weight, preferred_element_type=jnp.float32)  7.65 us
  transfers between devices with their start and end apart: 4, of which 4 were waited for; matrix products, arithmetic and copies ran while one was open for 1% of the time, Pallas kernels for 0%

commit v1 on v0

--- a/solution.py
+++ b/solution.py
@@ -91,7 +91,15 @@
         )
 
     full_keys, full_values = (
-        lax.all_to_all(spread(cache_keys), "tensor", split_axis=2, concat_axis=1, tiled=True),
+        jnp.concatenate(
+            lax.all_to_all(
+                jnp.stack(jnp.split(spread(cache_keys), lax.axis_size("tensor"), axis=2)),
+                axis_name="tensor",
+                split_axis=0,
+                concat_axis=0,
+            ),
+            axis=1,
+        ),
         lax.all_to_all(spread(cache_values), "tensor", split_axis=2, concat_axis=1, tiled=True),
     )
     kv_first = my_rank * local_heads // group_heads

time: 297 us -> 294 us (0.990)
  the two profiles are of different devices: /device:TPU:8 before, /device:TPU:18 now
where the time goes in v1:
time: 294 us; the launch traced here: 293 us
  waiting for transfers between devices  212 us (72%)
  local copies, waits for them, and re-layouts  33.6 us (11%)
  starting transfers between devices  15.4 us (5%)
  between operations  13.7 us (5%)
  matrix products  12.5 us (4%)
  other arithmetic  5.59 us (2%)
    all_gather x1, waiting for transfers between devices, body(): home_all = lax.all_gather(attended_rows, 'dp', axis=0, tiled=True)  99.2 us
    reduce_scatter x1, waiting for transfers between devices, body(): lax.psum_scatter(jnp.dot(picked, out_weight, preferred_element_type=jnp.f...  64.8 us
    all_to_all x1, waiting for transfers between devices, body(): lax.all_to_all(spread(cache_values), 'tensor', split_axis=2, concat_axis=...  24.7 us
    all_to_all x1, waiting for transfers between devices, body(): lax.all_to_all(jnp.stack(jnp.split(spread(cache_keys), lax.axis_size('ten...  23.5 us
    gather x1, local copies, waits for them, and re-layouts, body(): picked = jnp.take(home_all, request * DRAFT + within, axis=0)  20.4 us
    all_to_all x1, starting transfers between devices, body(): lax.all_to_all(spread(cache_values), 'tensor', split_axis=2, concat_axis=...  10.4 us
    dot_general x1, matrix products, body(): jnp.dot(picked, out_weight, preferred_element_type=jnp.float32)  7.67 us
  transfers between devices with their start and end apart: 4, of which 4 were waited for; matrix products, arithmetic and copies ran while one was open for 1% of the time, Pallas kernels for 0%

profile of v1, /device:TPU:18, one launch (start us, length us, event | category | flops | bytes accessed | tf_op | source)
XLA Modules:
  0.0 293.3 jit_solution(9980169149079549998)
XLA Ops:
  6.5 1.3 copy_bitcast_fusion.4
  7.8 1.2 broadcast_in_dim.101
  9.0 10.4 %all-to-all-start = ((bf16[2,128,16,128]{3,1,0,2:T(8,128)(2,1)}), bf16[2,128,16,128]{3,1,0,2:T(8,128)(2,1)S(1)}, u32[]{:S(2)}, u32[]{:S(2)}) async-start(bf16[2,128,16,128]{3,1,0,2:T(8,128)(2,1)} %bitcast.20), calls=%async_computation | async-start | bytes 2097152 | tf_op jit(solution)/shard_map/all_to_all | solution.py:103
  19.5 0.1 copy_bitcast_fusion.3
  19.6 0.3 broadcast_in_dim.102
  20.3 1.0 copy-done.1
  21.3 24.7 %all-to-all-done = bf16[2,128,16,128]{3,1,0,2:T(8,128)(2,1)S(1)} async-done(((bf16[2,128,16,128]{3,1,0,2:T(8,128)(2,1)}), bf16[2,128,16,128]{3,1,0,2:T(8,128)(2,1)S(1)}, u32[]{:S(2)}, u32[]{:S(2)}) %all-to-all-start) | async-done | bytes 1048608 | tf_op jit(solution)/shard_map/all_to_all | solution.py:103
  46.0 4.9 %all-to-all-start.1 = ((bf16[16,2,128,1,128]{4,2,1,3,0:T(8,128)(2,1)}), bf16[16,2,128,1,128]{4,2,1,3,0:T(8,128)(2,1)S(1)}, u32[]{:S(2)}, u32[]{:S(2)}) async-start(bf16[16,2,128,1,128]{4,2,1,3,0:T(8,128)(2,1)} %copy-done.1), calls=%async_computation.1 | async-start | bytes 2097152 | tf_op jit(solution)/shard_map/all_to_all | solution.py:95
  51.0 1.0 copy.79
  52.0 0.1 dynamic_slice.34
  52.1 0.8 constant_dynamic-slice_fusion.1
  52.9 1.0 copy.66
  53.9 23.5 %all-to-all-done.1 = bf16[16,2,128,1,128]{4,2,1,3,0:T(8,128)(2,1)S(1)} async-done(((bf16[16,2,128,1,128]{4,2,1,3,0:T(8,128)(2,1)}), bf16[16,2,128,1,128]{4,2,1,3,0:T(8,128)(2,1)S(1)}, u32[]{:S(2)}, u32[]{:S(2)}) %all-to-all-start.1) | async-done | bytes 1048608 | tf_op jit(solution)/shard_map/all_to_all | solution.py:95
  77.4 0.1 copy.68
  77.5 14.1 %while.10 = (s32[]{:T(128)}, bf16[2,64,1,8,128]{4,3,1,0,2:T(8,128)(2,1)}, s32[2]{0:T(128)S(1)}, bf16[2,2048,1,128]{3,1,2,0:T(8,128)(2,1)}, s32[2]{0:T(128)S(1)},...) while((s32[]{:T(128)}, ...), condition=%wide.region_8.9_spmd, body=%wide.region_3.8_spmd.sunk | while | flops 566699072 | bytes 21984120 | solution.py:114
  77.5 0.7 dynamic_slice.73
  78.2 0.6 iota_compare_fusion.6
  78.8 0.7 dynamic_slice.72
  79.5 0.6 iota_compare_fusion.5
  80.1 0.1 fusion.85
  80.2 0.3 fusion.86
  80.5 0.9 bitcast_reduce_fusion.2
  81.4 0.1 fusion.88
  81.5 1.0 fusion.87
  82.4 1.1 fusion.89
  83.5 0.2 fusion.90
  83.8 0.1 copy_dynamic-update-slice_fusion.2
  83.9 0.7 copy-done.5
  84.6 0.6 dynamic_slice.73
  85.2 0.6 iota_compare_fusion.6
  85.9 0.7 dynamic_slice.72
  86.5 0.6 iota_compare_fusion.5
  87.2 0.1 fusion.85
  87.3 0.3 fusion.86
  87.5 0.9 bitcast_reduce_fusion.2
  88.4 0.1 fusion.88
  88.5 1.0 fusion.87
  89.5 1.1 fusion.89
  90.5 0.2 fusion.90
  90.8 0.1 copy_dynamic-update-slice_fusion.2
  90.9 0.7 copy-done.5
  91.6 1.7 copy.92
  93.5 0.4 fusion.66
  93.8 0.4 select_reduce_fusion
  94.3 99.2 %all-gather.2.cloned.1.call-done = bf16[4096,1024]{1,0:T(8,128)(2,1)} async-done(((bf16[128,1024]{1,0:T(8,128)(2,1)}), bf16[4096,1024]{1,0:T(8,128)(2,1)}) %all-gather.2.cloned.1.call-update) | async-done | bytes 8388624 | tf_op jit(solution)/shard_map/all_gather | solution.py:121
  193.5 20.4 %gather_fusion = bf16[3072,1024]{1,0:T(8,128)(2,1)} fusion(bf16[4096,1024]{1,0:T(8,128)(2,1)} %all-gather.2.cloned.1.call-done, s32[3072]{0:T(1024)S(1)} %broadcast_clamp_fusion), kind=kCustom, calls=%fused_computation | custom fusion | bytes 12595200 | tf_op jit(solution)/shard_map/jit(_take)/gather | solution.py:124
  213.9 7.7 %fusion.34 = bf16[3072,512]{1,0:T(8,128)(2,1)} fusion(bf16[1024,512]{1,0:T(8,128)(2,1)S(1)} %copy-done, bf16[3072,1024]{1,0:T(8,128)(2,1)} %gather_fusion, pred[3072]{0:T(1024)(128)(4,1)S(1)} %compare_and_fusion.1, pred[3072]{0:T(1024)(128)(4,1)S(1)} %fusion.66), kind=kOutput, calls=%fused_computation.49 | convolution fusion | flops 3229089792 | bytes 10491904 | tf_op jit(solution)/shard_map/dot_general | solution.py:127
  221.6 64.8 %reduce-scatter.2.cloned.1.call-done = bf16[192,512]{1,0:T(8,128)(2,1)} async-done(((bf16[3072,512]{1,0:T(8,128)(2,1)}), bf16[192,512]{1,0:T(8,128)(2,1)}) %reduce-scatter.2.cloned.1.call-update) | async-done | bytes 196624 | tf_op jit(solution)/shard_map/reduce_scatter | solution.py:126
  (56 shorter events, 0.5 us)
Async XLA Ops:
  6.5 207.4 %copy-start = (bf16[1024,512]{1,0:T(8,128)(2,1)S(1)}, bf16[1024,512]{1,0:T(8,128)(2,1)}, u32[]{:S(2)}) copy-start(bf16[1024,512]{1,0:T(8,128)(2,1)} %param.17) | copy-start | bytes 3145732
  6.5 12.9 %copy-start.3 = (bf16[2,128,1024]{2,1,0:T(8,128)(2,1)S(1)}, bf16[2,128,1024]{2,1,0:T(8,128)(2,1)}, u32[]{:S(2)}) copy-start(bf16[2,128,1024]{2,1,0:T(8,128)(2,1)} %param.15) | copy-start | bytes 1572868
  9.0 36.9 %all-to-all-start = ((bf16[2,128,16,128]{3,1,0,2:T(8,128)(2,1)}), bf16[2,128,16,128]{3,1,0,2:T(8,128)(2,1)S(1)}, u32[]{:S(2)}, u32[]{:S(2)}) async-start(bf16[2,128,16,128]{3,1,0,2:T(8,128)(2,1)} %bitcast.20), calls=%async_computation | async-start | bytes 2097152 | tf_op jit(solution)/shard_map/all_to_all | solution.py:103
  19.5 32.5 %copy-start.9 = (s32[64]{0:T(128)S(1)}, s32[64]{0:T(128)}, u32[]{:S(2)}) copy-start(s32[64]{0:T(128)} %param.19) | copy-start | bytes 772
  20.0 57.5 %copy-start.8 = (s32[2]{0:T(128)S(1)}, s32[2]{0:T(128)}, u32[]{:S(2)}) copy-start(s32[2]{0:T(128)} %param.18) | copy-start | bytes 28
  20.2 1.0 copy-start.1
  46.0 31.4 %all-to-all-start.1 = ((bf16[16,2,128,1,128]{4,2,1,3,0:T(8,128)(2,1)}), bf16[16,2,128,1,128]{4,2,1,3,0:T(8,128)(2,1)S(1)}, u32[]{:S(2)}, u32[]{:S(2)}) async-start(bf16[16,2,128,1,128]{4,2,1,3,0:T(8,128)(2,1)} %copy-done.1), calls=%async_computation.1 | async-start | bytes 2097152 | tf_op jit(solution)/shard_map/all_to_all | solution.py:95
  50.9 142.6 %all-gather.2.cloned.1.call-start = ((), (), s32[]{:S(2)}) async-start(), calls=%async_computation.3 | async-start | bytes 8650752 | tf_op jit(solution)/shard_map/all_gather | solution.py:121
  77.5 15.9 %copy-start.6 = (s32[64]{0:T(128)S(1)}, s32[64]{0:T(128)}, u32[]{:S(2)}) copy-start(s32[64]{0:T(128)} %param.21) | copy-start | bytes 772
  77.5 15.9 %copy-start.7 = (s32[64]{0:T(128)S(1)}, s32[64]{0:T(128)}, u32[]{:S(2)}) copy-start(s32[64]{0:T(128)} %param.20) | copy-start | bytes 772
  80.5 1.9 copy-start.2
  82.4 1.3 copy-start.4
  83.9 0.7 copy-start.5
  87.5 1.9 copy-start.2
  89.4 1.3 copy-start.4
  90.9 0.7 copy-start.5
  93.4 193.1 %reduce-scatter.2.cloned.1.call-start = ((), (), s32[]{:S(2)}) async-start(), calls=%async_computation.4 | async-start | bytes 3342336 | tf_op jit(solution)/shard_map/reduce_scatter | solution.py:126
Sparse Core Ops, SparseCore 0:
  93.5 99.9 all-gather.1
  221.7 64.6 reduce-scatter.1
